TPU v7x, 32 devices: a whole 2x2x4 slice. The times are simulated.
32 devices in a mesh: out: 8 (over z, x), inp: 4 (over y, core).
Axes of the slice: x: 2, y: 2, z: 4, core: 2. Of those that a mesh axis runs over, the one named last changes fastest.
Arguments:
- tensor: bfloat16 [1024, 1024, 1024], P('out', 'inp'), may hold values from -0.005859375 to 0.005859375
- state: bfloat16 [768, 1024], P('out'), may hold values from -6 to 6
Outputs:
- collision: bfloat16 [768, 1024], P('inp', 'out')
All inputs are finite; a program needn't handle non-finite values.
Results may differ from a plain program's by a relative error of at most 0.001.
Values may be sent and summed in bfloat16 or wider, within the bound.
A program may use at most 128 MiB of HBM per device.

v0:
```python
import jax
import jax.numpy as jnp
from jax import lax
from jax.sharding import PartitionSpec as P


def local(tensor, state):
    rows_out = tensor.shape[0]
    rows_inp = tensor.shape[1]
    width = tensor.shape[2]
    flat = tensor.reshape(rows_out * rows_inp, width)
    first_col = lax.axis_index("inp") * rows_inp
    piece = lax.all_gather(state, "out", axis=0, tiled=True)
    inner = lax.dot_general(
        piece, flat, (((1,), (1,)), ((), ())), preferred_element_type=jnp.float32
    )
    inner = inner.reshape(piece.shape[0], rows_out, rows_inp)
    chosen = lax.dynamic_slice_in_dim(piece, first_col, rows_inp, 1).astype(jnp.float32)
    partial_sum = jnp.sum(inner * chosen[:, None, :], axis=2)
    owned = lax.psum_scatter(partial_sum, "inp", scatter_dimension=0, tiled=True)
    return owned.astype(jnp.bfloat16)


def solution(mesh):
    placed = (P("out", "inp", None), P("out", None))
    return jax.shard_map(
        local, mesh=mesh, in_specs=placed, out_specs=P("inp", "out"), check_vma=False
    )
```

profile of v0, /device:TPU:0, one launch (start us, length us, event | category | flops | bytes accessed | tf_op | source)
XLA Modules:
  0.0 146.9 jit_solution(9233174708893492193)
XLA Ops:
  6.5 0.0 all-gather.2.cloned.1.call-start
  6.5 0.7 all-gather.2.cloned.1.call-update
  7.3 0.0 reduce-scatter.4.cloned.1.call-start
  7.3 49.1 %all-gather.2.cloned.1.call-done = bf16[768,1024]{1,0:T(8,128)(2,1)} async-done(((bf16[96,1024]{1,0:T(8,128)(2,1)}), bf16[768,1024]{1,0:T(8,128)(2,1)}) %all-gather.2.cloned.1.call-update) | async-done | bytes 1572880 | tf_op jit(solution)/shard_map/all_gather | solution.py:13
  56.4 1.0 dynamic-slice_convert_fusion
  57.5 0.3 copy.8
  57.8 60.4 %multiply_reduce_fusion = f32[768,128]{0,1:T(8,128)S(1)} fusion(f32[768,256]{0,1:T(8,128)S(1)} %copy.8, bf16[128,256,1024]{2,1,0:T(8,128)(2,1)} %param.2, bf16[768,1024]{1,0:T(8,128)(2,1)} %all-gather.2.cloned.1.call-done), kind=kOutput, calls=%fused_computation | convolution fusion | flops 51589840896 | bytes 69861376 | tf_op jit(solution)/shard_map/dot_general | solution.py:14
  118.2 0.9 copy.10
  119.1 0.0 reduce-scatter.4.cloned.1.call-update
  119.1 19.3 %reduce-scatter.4.cloned.1.call-done = f32[192,128]{1,0:T(8,128)} async-done(((f32[768,128]{1,0:T(8,128)}), f32[192,128]{1,0:T(8,128)}) %reduce-scatter.4.cloned.1.call-update) | async-done | bytes 98320 | tf_op jit(solution)/shard_map/reduce_scatter | solution.py:20
  138.5 1.5 %convert_element_type.7 = bf16[192,128]{1,0:T(8,128)(2,1)} convert(f32[192,128]{1,0:T(8,128)} %reduce-scatter.4.cloned.1.call-done) | non-fusion elementwise | flops 24576 | bytes 147456 | tf_op jit(solution)/shard_map/convert_element_type | solution.py:21
Async XLA Ops:
  6.5 49.9 %all-gather.2.cloned.1.call-start = ((), (), s32[]{:S(2)}) async-start(), calls=%async_computation.1 | async-start | bytes 1769472 | tf_op jit(solution)/shard_map/all_gather | solution.py:13
  7.3 131.2 %reduce-scatter.4.cloned.1.call-start = ((), (), s32[]{:S(2)}) async-start(), calls=%async_computation.2 | async-start | bytes 491520 | tf_op jit(solution)/shard_map/reduce_scatter | solution.py:20
Sparse Core Ops, SparseCore 0:
  9.5 46.8 all-gather.1
  119.3 19.1 reduce-scatter.3
where the time goes:
time: 147 us
  waiting for transfers between devices  69.2 us (47%)
  matrix products  60.4 us (41%)
  between operations  13.4 us (9%)
  other arithmetic  2.56 us (2%)
    dot_general x1, matrix products, local(): lax.dot_general(piece, flat, (((1,), (1,)), ((), ())), preferred_element_...  60.4 us
    all_gather x1, waiting for transfers between devices, local(): piece = lax.all_gather(state, 'out', axis=0, tiled=True)  49.1 us
    reduce_scatter x1, waiting for transfers between devices, local(): lax.psum_scatter(partial_sum, 'inp', scatter_dimension=0, tiled=True)  19.3 us
  transfers between devices with their start and end apart: 2, of which 2 were waited for; matrix products, arithmetic and copies ran while one was open for 0% of the time, Pallas kernels for 0%

commit v1 on v0

--- a/solution.py
+++ b/solution.py
@@ -10,7 +10,9 @@
     width = tensor.shape[2]
     flat = tensor.reshape(rows_out * rows_inp, width)
     first_col = lax.axis_index("inp") * rows_inp
-    piece = lax.all_gather(state, "out", axis=0, tiled=True)
+    piece = jnp.concatenate(
+        lax.all_to_all(jnp.stack([state] * lax.axis_size("out")), "out", 0, 0), axis=0
+    )
     inner = lax.dot_general(
         piece, flat, (((1,), (1,)), ((), ())), preferred_element_type=jnp.float32
     )

time: 147 us -> 143 us (0.973)
  waiting for transfers between devices: 69.2 us -> 57 us
  starting transfers between devices: 0.04 us -> 7.32 us
  local copies, waits for them, and re-layouts: 1.17 us -> 3.44 us
    all_gather x1 -> x0, waiting for transfers between devices: 49.1 us -> none  [local(): piece = lax.all_gather(state, 'out', axis=0, tiled=True)]
    all_to_all x0 -> x1, waiting for transfers between devices: none -> 37 us  [local(): lax.all_to_all(jnp.stack([state] * lax.axis_size('out')), 'out', 0, 0)]
    all_to_all x0 -> x1, starting transfers between devices: none -> 7.28 us  [local(): lax.all_to_all(jnp.stack([state] * lax.axis_size('out')), 'out', 0, 0)]
    another operation x0 -> x1, local copies, waits for them, and re-layouts: none -> 2.27 us  [local(): jnp.stack([state] * lax.axis_size('out'))]
where the time goes in v1:
time: 143 us
  matrix products  60 us (42%)
  waiting for transfers between devices  57 us (40%)
  between operations  13.4 us (9%)
  starting transfers between devices  7.32 us (5%)
  local copies, waits for them, and re-layouts  3.44 us (2%)
  other arithmetic  1.58 us (1%)
    dot_general x1, matrix products, local(): lax.dot_general(piece, flat, (((1,), (1,)), ((), ())), preferred_element_...  60 us
    all_to_all x1, waiting for transfers between devices, local(): lax.all_to_all(jnp.stack([state] * lax.axis_size('out')), 'out', 0, 0)  37 us
    reduce_scatter x1, waiting for transfers between devices, local(): lax.psum_scatter(partial_sum, 'inp', scatter_dimension=0, tiled=True)  20 us
    all_to_all x1, starting transfers between devices, local(): lax.all_to_all(jnp.stack([state] * lax.axis_size('out')), 'out', 0, 0)  7.28 us
  transfers between devices with their start and end apart: 2, of which 2 were waited for; matrix products, arithmetic and copies ran while one was open for 0% of the time, Pallas kernels for 0%

profile of v1, /device:TPU:0, one launch (start us, length us, event | category | flops | bytes accessed | tf_op | source)
XLA Modules:
  0.0 142.8 jit_solution(1464231651176460217)
XLA Ops:
  6.5 2.3 %stack.2 = bf16[8,96,1024]{2,1,0:T(8,128)(2,1)} broadcast(bf16[96,1024]{1,0:T(8,128)(2,1)} %param.3), dimensions={1,2} | broadcast | bytes 1769472 | tf_op jit(solution)/shard_map/stack | solution.py:14
  8.8 7.3 %all-to-all-start = ((bf16[8,96,1024]{2,1,0:T(8,128)(2,1)}), bf16[8,96,1024]{2,1,0:T(8,128)(2,1)S(1)}, u32[]{:S(2)}, u32[]{:S(2)}) async-start(bf16[8,96,1024]{2,1,0:T(8,128)(2,1)} %stack.2), calls=%async_computation | async-start | bytes 3145728 | tf_op jit(solution)/shard_map/all_to_all | solution.py:14
  16.1 0.0 reduce-scatter.4.cloned.1.call-start
  16.1 37.0 %all-to-all-done = bf16[8,96,1024]{2,1,0:T(8,128)(2,1)S(1)} async-done(((bf16[8,96,1024]{2,1,0:T(8,128)(2,1)}), bf16[8,96,1024]{2,1,0:T(8,128)(2,1)S(1)}, u32[]{:S(2)}, u32[]{:S(2)}) %all-to-all-start) | async-done | bytes 1572896 | tf_op jit(solution)/shard_map/all_to_all | solution.py:14
  53.1 0.1 dynamic-slice_convert_fusion
  53.2 0.3 copy.8
  53.4 60.0 %multiply_reduce_fusion = f32[768,128]{0,1:T(8,128)S(1)} fusion(f32[768,256]{0,1:T(8,128)S(1)} %copy.8, bf16[768,1024,1]{1,0,2:T(8,128)(2,1)S(1)} %bitcast.7, bf16[128,256,1024]{2,1,0:T(8,128)(2,1)} %param.2), kind=kOutput, calls=%fused_computation | convolution fusion | flops 51589840896 | bytes 69861376 | tf_op jit(solution)/shard_map/dot_general | solution.py:16
  113.4 0.9 copy.10
  114.3 0.0 reduce-scatter.4.cloned.1.call-update
  114.4 20.0 %reduce-scatter.4.cloned.1.call-done = f32[192,128]{1,0:T(8,128)} async-done(((f32[768,128]{1,0:T(8,128)}), f32[192,128]{1,0:T(8,128)}) %reduce-scatter.4.cloned.1.call-update) | async-done | bytes 98320 | tf_op jit(solution)/shard_map/reduce_scatter | solution.py:22
  134.4 1.5 %convert_element_type.7 = bf16[192,128]{1,0:T(8,128)(2,1)} convert(f32[192,128]{1,0:T(8,128)} %reduce-scatter.4.cloned.1.call-done) | non-fusion elementwise | flops 24576 | bytes 147456 | tf_op jit(solution)/shard_map/convert_element_type | solution.py:23
Async XLA Ops:
  8.8 44.3 %all-to-all-start = ((bf16[8,96,1024]{2,1,0:T(8,128)(2,1)}), bf16[8,96,1024]{2,1,0:T(8,128)(2,1)S(1)}, u32[]{:S(2)}, u32[]{:S(2)}) async-start(bf16[8,96,1024]{2,1,0:T(8,128)(2,1)} %stack.2), calls=%async_computation | async-start | bytes 3145728 | tf_op jit(solution)/shard_map/all_to_all | solution.py:14
  16.1 118.3 %reduce-scatter.4.cloned.1.call-start = ((), (), s32[]{:S(2)}) async-start(), calls=%async_computation.2 | async-start | bytes 491520 | tf_op jit(solution)/shard_map/reduce_scatter | solution.py:22
Sparse Core Ops, SparseCore 0:
  114.5 19.8 reduce-scatter.3
